TPU v7x, 32 devices: a whole 2x2x4 slice. The times are simulated.
32 devices in a mesh: grid: 8 (over z, x), orb: 4 (over y, core).
Axes of the slice: x: 2, y: 2, z: 4, core: 2. Of those that a mesh axis runs over, the one named last changes fastest.
Arguments:
- orbitals: bfloat16 [1800, 65536], P('orb', 'grid'), may hold values from -0.5 to 1.5
- pivots: int32 [3, 96], replicated, may hold values from 0 to 65535, as said below
Outputs:
- cholesky_factor: float32 [65536, 288], P(('grid', 'orb'))
- residual_diagonal: float32 [65536], P(('grid', 'orb'))
- diagonal_peaks: float32 [3], replicated
Inputs may be any that keep to these rules, and one draw needn't show every extreme that they name: `pivots`: all 3 x 96 pivot indices are distinct grid points.
All inputs are finite; a program needn't handle non-finite values.
Results may differ from a plain program's by a relative error of at most 0.0003.
Values may be sent and summed in bfloat16 or wider, within the bound.
A program may use at most 64 MiB of HBM per device.

v0:
```python
import functools

import jax
import jax.numpy as jnp
from jax import lax
from jax.experimental import pallas as pl
from jax.experimental.pallas import tpu as pltpu
from jax.sharding import PartitionSpec as P

F32 = jnp.float32
BF16 = jnp.bfloat16
HIGHEST = lax.Precision.HIGHEST
MESH = pl.DeviceIdType.MESH
BLOCK = 48
PARTS = 4


def dot_nn(a, b, precision=None):
    return lax.dot_general(
        a, b, (((1,), (0,)), ((), ())), precision=precision, preferred_element_type=F32
    )


def dot_nt(a, b, precision=None):
    return lax.dot_general(
        a, b, (((1,), (1,)), ((), ())), precision=precision, preferred_element_type=F32
    )


def dot_tn(a, b, precision=None):
    return lax.dot_general(
        a, b, (((0,), (0,)), ((), ())), precision=precision, preferred_element_type=F32
    )


def eliminate_small(t, size):
    row_at = lax.broadcasted_iota(jnp.int32, t.shape, 0)
    for k in range(size):
        scale = lax.rsqrt(t[k : k + 1, k : k + 1])
        row = t[k : k + 1, :] * scale
        column = t[:, k : k + 1] * scale
        t = jnp.where(row_at > k, t - column * row, jnp.where(row_at == k, row, t))
    return t


def kernel(
    n_grid, n_orb, steps, orbitals_count,
    orb_hbm, piv_ref,
    factor_hbm, diag_ref, peaks_ref,
    own, other, mine, total, heard, swap, sums, arrived, side_sums, side_arrived, local, pair_send, pair_recv,
    aug, out_v, tile_mine, tile_orb, tile_grid,
    load_sem, out_sem, x_send, x_recv, p1_send, p1_recv, p2_send, p2_recv,
    c_send, c_recv, q_send, q_recv, h_send, h_recv, s_send, s_recv, z_send, z_recv,
    mo_send, mo_recv, mg_send, mg_recv,
):
    g = lax.axis_index("grid")
    o = lax.axis_index("orb")
    core = lax.rem(o, 2)
    side = o // 2
    mate = o + 1 - 2 * core
    across = (1 - side) * 2 + core
    share = own.shape[2]
    slots, slot_rows, _ = mine.shape
    rank = slots * slot_rows
    part = share // PARTS
    rows = share * n_orb

    loads = []
    for b in range(n_orb):
        copy = pltpu.make_async_copy(
            orb_hbm.at[:, pl.ds(b * share, share)], own.at[b], load_sem.at[b]
        )
        copy.start()
        loads.append(copy)

    barrier = pltpu.get_barrier_semaphore()
    for d in range(1, n_grid):
        pl.semaphore_signal(
            barrier, inc=1, device_id=(lax.rem(g + d, n_grid), o), device_id_type=MESH
        )
    for d in range(1, n_orb):
        pl.semaphore_signal(
            barrier, inc=1, device_id=(g, lax.rem(o + d, n_orb)), device_id_type=MESH
        )
    pl.semaphore_wait(barrier, n_grid + n_orb - 2)

    crossing = []
    for yy in range(2):
        start = pl.multiple_of((yy * 2 + 1 - core) * share, share)
        copy = pltpu.make_async_remote_copy(
            src_ref=orb_hbm.at[:, pl.ds(start, share)],
            dst_ref=other.at[yy],
            send_sem=x_send.at[yy],
            recv_sem=x_recv.at[yy],
            device_id=(g, mate),
            device_id_type=MESH,
        )
        copy.start()
        crossing.append(copy)

    base = g * rows
    wanted = piv_ref[...] - base
    picked = None
    for b in range(n_orb):
        loads[b].wait()
        lanes = lax.broadcasted_iota(jnp.int32, (rank, share), 1) + b * share
        hot = jnp.where(lanes == wanted, 1.0, 0.0).astype(BF16)
        term = dot_nt(hot, own[b])
        picked = term if picked is None else picked + term
    picked = picked.astype(BF16)
    for s in range(slots):
        mine[s] = picked[s * slot_rows : (s + 1) * slot_rows]

    def first(d):
        target = lax.rem(g + d, n_grid)
        return target, pltpu.make_async_remote_copy(
            src_ref=mine.at[lax.rem(target, slots)],
            dst_ref=heard.at[d],
            send_sem=p1_send.at[d],
            recv_sem=p1_recv.at[d],
            device_id=(target, o),
            device_id_type=MESH,
        )

    def second(d):
        target = lax.rem(g + d, n_grid)
        return pltpu.make_async_remote_copy(
            src_ref=heard.at[0],
            dst_ref=total.at[lax.rem(g, slots)],
            send_sem=p2_send.at[d],
            recv_sem=p2_recv.at[d],
            device_id=(target, o),
            device_id_type=MESH,
        )

    for d in range(1, n_grid):
        target, copy = first(d)

        @pl.when(target < slots)
        def _(copy=copy):
            copy.start()

    @pl.when(g < slots)
    def _():
        added = mine[lax.rem(g, slots)]
        for d in range(1, n_grid):
            first(d)[1].wait_recv()
            added = added + heard[d]
        heard[0] = added
        for d in range(1, n_grid):
            second(d).start()
        total[lax.rem(g, slots)] = added

    for copy in crossing:
        copy.wait_recv()

    def moments(block, yy, p):
        lo = p * part
        a = own[block, :, lo : lo + part]
        b = other[yy, :, lo : lo + part]
        a32 = a.astype(F32)
        b32 = b.astype(F32)
        squares = jnp.sum(a32 * a32, axis=0, keepdims=True) + jnp.sum(
            b32 * b32, axis=0, keepdims=True
        )
        point_sum = jnp.sum(a32, axis=0, keepdims=True) + jnp.sum(b32, axis=0, keepdims=True)
        return squares, point_sum

    for p in range(PARTS):
        squares, point_sum = moments(across, 1 - side, p)
        side_sums[p] = jnp.zeros((8, part), F32)
        side_sums[p, 0:1] = squares
        side_sums[p, 1:2] = point_sum
        squares, _ = moments(o, side, p)
        local[p, rank : rank + 8, :] = jnp.broadcast_to(squares, (8, part))

    for d in range(1, n_grid):
        source = lax.rem(g + n_grid - d, n_grid)

        @pl.when(source < slots)
        def _(d=d):
            second(d).wait_recv()

    swap_copy = pltpu.make_async_remote_copy(
        src_ref=total, dst_ref=swap, send_sem=c_send, recv_sem=c_recv,
        device_id=(g, mate), device_id_type=MESH,
    )
    swap_copy.start()
    here = jnp.reshape(total[...], (rank, total.shape[2]))
    pair_here = dot_nt(here, here)
    swap_copy.wait_recv()
    there = jnp.reshape(swap[...], (rank, swap.shape[2]))
    pair = pair_here + dot_nt(there, there)
    half = rank // 2
    pivot_mean = (
        jnp.sum(here.astype(F32), axis=1, keepdims=True)
        + jnp.sum(there.astype(F32), axis=1, keepdims=True)
    ) / (2.0 * total.shape[2])
    for h in range(2):
        pair_send[h, :, 0:rank] = pair[h * half : (h + 1) * half]
        pair_send[h, :, rank : rank + 1] = pivot_mean[h * half : (h + 1) * half]
    pair_copy = pltpu.make_async_remote_copy(
        src_ref=pair_send.at[core], dst_ref=pair_recv.at[0], send_sem=q_send, recv_sem=q_recv,
        device_id=(g, across), device_id_type=MESH,
    )
    pair_copy.start()

    def products(block, yy, p):
        lo = p * part
        a = own[block, :, lo : lo + part]
        b = other[yy, :, lo : lo + part]
        return dot_nn(here, a) + dot_nn(there, b)


    travel = []
    for p in range(PARTS):
        inner = products(across, 1 - side, p)
        squares = side_sums[p, 0:1]
        point_sum = side_sums[p, 1:2]
        rest = inner - pivot_mean * point_sum
        most = jnp.max(jnp.abs(rest), axis=0, keepdims=True)
        step = jnp.maximum(most * (1.0 / 32767.0), 1e-30)
        coded = jnp.round(rest * (1.0 / step))
        sums[p] = jnp.clip(coded, -32767.0, 32767.0).astype(jnp.int32).astype(jnp.int16)
        side_sums[p, 2:3] = step
        for copy in (
            pltpu.make_async_remote_copy(
                src_ref=side_sums.at[p], dst_ref=side_arrived.at[p],
                send_sem=z_send.at[p], recv_sem=z_recv.at[p],
                device_id=(g, across), device_id_type=MESH,
            ),
            pltpu.make_async_remote_copy(
                src_ref=sums.at[p], dst_ref=arrived.at[p],
                send_sem=s_send.at[p], recv_sem=s_recv.at[p],
                device_id=(g, across), device_id_type=MESH,
            ),
        ):
            copy.start()
            travel.append(copy)

    pair_copy.wait_recv()
    half_copy = pltpu.make_async_remote_copy(
        src_ref=pair_recv.at[0], dst_ref=pair_recv.at[1], send_sem=h_send, recv_sem=h_recv,
        device_id=(g, mate), device_id_type=MESH,
    )
    half_copy.start()
    for p in range(PARTS):
        local[p, 0:rank, :] = products(o, side, p)
    half_copy.wait_recv()
    first_half = jnp.where(core == 0, pair_recv[0], pair_recv[1])
    second_half = jnp.where(core == 0, pair_recv[1], pair_recv[0])
    wide = aug.shape[1]
    aug[...] = jnp.zeros((rank, wide), F32)
    aug[0:half, 0:rank] = jnp.square((pair_send[0] + first_half)[:, 0:rank] / orbitals_count)
    aug[half:rank, 0:rank] = jnp.square((pair_send[1] + second_half)[:, 0:rank] / orbitals_count)
    far_mean = jnp.concatenate(
        [first_half[:, rank : rank + 1], second_half[:, rank : rank + 1]], axis=0
    )

    def block_step(j, carry):
        start = pl.multiple_of(j * BLOCK, BLOCK)
        strip = aug[pl.ds(start, BLOCK), :]
        pick = jnp.where(
            lax.broadcasted_iota(jnp.int32, (wide, 128), 0)
            == lax.broadcasted_iota(jnp.int32, (wide, 128), 1) + start,
            1.0,
            0.0,
        )
        lane = lax.broadcasted_iota(jnp.int32, (BLOCK, 128), 1)
        row_at = lax.broadcasted_iota(jnp.int32, (BLOCK, 128), 0)
        square = dot_nn(strip, pick, HIGHEST)
        tile = jnp.where(lane < BLOCK, square, jnp.where(lane == row_at + 64, 1.0, 0.0))
        tile = eliminate_small(tile, BLOCK)
        inverse = tile[:, 64 : 64 + BLOCK]
        at = lax.broadcasted_iota(jnp.int32, (BLOCK, wide), 1)
        unit = jnp.where(at == lax.broadcasted_iota(jnp.int32, (BLOCK, wide), 0) + start, 1.0, 0.0)
        solved = dot_nn(
            inverse, jnp.where((at >= start) & (at < start + BLOCK), unit, strip), HIGHEST
        )
        multipliers = jnp.where(at >= start + BLOCK, solved, 0.0)
        every_lane = lax.broadcasted_iota(jnp.int32, (rank, wide), 1)
        every_row = lax.broadcasted_iota(jnp.int32, (rank, wide), 0)
        clear = (
            (every_lane >= start) & (every_lane < start + BLOCK) & (every_row >= start + BLOCK)
        )
        aug[...] = jnp.where(clear, 0.0, aug[...]) - dot_tn(multipliers, solved, HIGHEST)[0:rank]
        aug[pl.ds(start, BLOCK), :] = jnp.where(at < start + BLOCK, solved, 0.0)
        return carry

    lax.fori_loop(0, rank // BLOCK, block_step, 0)
    lower_inverse = aug[...]

    count = rank // steps
    best = [None] * steps
    stores = []
    for p in range(PARTS):
        travel[2 * p].wait_recv()
        travel[2 * p + 1].wait_recv()
        far = side_arrived[p]
        inner = (
            local[p, 0:rank, :]
            + arrived[p].astype(jnp.int32).astype(F32) * far[2:3]
            + far_mean * far[1:2]
        )
        columns = jnp.square(inner / orbitals_count)
        diagonal = jnp.square((local[p, rank : rank + 1, :] + far[0:1]) / orbitals_count)
        solved = dot_nn(lower_inverse[:, 0:rank], columns, HIGHEST)
        out_v[p] = solved.T
        store = pltpu.make_async_copy(
            out_v.at[p], factor_hbm.at[pl.ds(p * part, part), :], out_sem.at[p]
        )
        store.start()
        stores.append(store)
        for s in range(steps):
            piece = solved[s * count : (s + 1) * count]
            diagonal = diagonal - jnp.sum(piece * piece, axis=0, keepdims=True)
            best[s] = diagonal if best[s] is None else jnp.maximum(best[s], diagonal)
        diag_ref[:, p * part : (p + 1) * part] = diagonal

    row8 = lax.broadcasted_iota(jnp.int32, (8, 128), 0)
    tile = jnp.zeros((8, 128), F32)
    for s in range(steps):
        top = jnp.max(best[s], axis=1, keepdims=True)
        tile = jnp.where(row8 == s, jnp.broadcast_to(top, (8, 128)), tile)
    tile_mine[0] = tile
    round_orb = []
    for d in range(1, n_orb):
        copy = pltpu.make_async_remote_copy(
            src_ref=tile_mine.at[0], dst_ref=tile_orb.at[d],
            send_sem=mo_send.at[d], recv_sem=mo_recv.at[d],
            device_id=(g, lax.rem(o + d, n_orb)), device_id_type=MESH,
        )
        copy.start()
        round_orb.append(copy)
    for d in range(1, n_orb):
        round_orb[d - 1].wait_recv()
        tile = jnp.maximum(tile, tile_orb[d])
    tile_mine[1] = tile
    round_grid = []
    for d in range(1, n_grid):
        copy = pltpu.make_async_remote_copy(
            src_ref=tile_mine.at[1], dst_ref=tile_grid.at[d],
            send_sem=mg_send.at[d], recv_sem=mg_recv.at[d],
            device_id=(lax.rem(g + d, n_grid), o), device_id_type=MESH,
        )
        copy.start()
        round_grid.append(copy)
    for d in range(1, n_grid):
        round_grid[d - 1].wait_recv()
        tile = jnp.maximum(tile, tile_grid[d])
    peaks_ref[...] = tile

    for store in stores:
        store.wait()
    for d in range(1, n_grid):
        target, copy = first(d)

        @pl.when(target < slots)
        def _(copy=copy):
            copy.wait_send()

    @pl.when(g < slots)
    def _():
        for d in range(1, n_grid):
            second(d).wait_send()

    for copy in crossing + [swap_copy, pair_copy, half_copy] + travel + round_orb + round_grid:
        copy.wait_send()


def solution(mesh):
    n_grid, n_orb = mesh.shape["grid"], mesh.shape["orb"]
    assert n_orb == 4

    def on_device(orbitals, pivots):
        depth, rows = orbitals.shape
        steps, count = pivots.shape
        rank = steps * count
        share = rows // n_orb
        part = share // PARTS
        slot_rows = -(-rank // n_grid)
        slot_rows = -(-slot_rows // 16) * 16
        while rank % slot_rows:
            slot_rows += 16
        slots = rank // slot_rows
        wide = -(-rank // 128) * 128
        dma = pltpu.SemaphoreType.DMA
        vmem = pltpu.VMEM
        factor, diagonal, peaks = pl.pallas_call(
            functools.partial(kernel, n_grid, n_orb, steps, depth * n_orb),
            out_shape=(
                jax.ShapeDtypeStruct((share, rank), F32),
                jax.ShapeDtypeStruct((1, share), F32),
                jax.ShapeDtypeStruct((8, 128), F32),
            ),
            in_specs=[
                pl.BlockSpec(memory_space=pl.ANY),
                pl.BlockSpec(memory_space=vmem),
            ],
            out_specs=(
                pl.BlockSpec(memory_space=pl.ANY),
                pl.BlockSpec(memory_space=vmem),
                pl.BlockSpec(memory_space=vmem),
            ),
            scratch_shapes=[
                vmem((n_orb, depth, share), BF16),
                vmem((2, depth, share), BF16),
                vmem((slots, slot_rows, depth), BF16),
                vmem((slots, slot_rows, depth), BF16),
                vmem((n_grid, slot_rows, depth), BF16),
                vmem((slots, slot_rows, depth), BF16),
                vmem((PARTS, rank, part), jnp.int16),
                vmem((PARTS, rank, part), jnp.int16),
                vmem((PARTS, 8, part), F32),
                vmem((PARTS, 8, part), F32),
                vmem((PARTS, rank + 8, part), F32),
                vmem((2, rank // 2, rank + 1), F32),
                vmem((2, rank // 2, rank + 1), F32),
                vmem((rank, wide), F32),
                vmem((PARTS, part, rank), F32),
                vmem((2, 8, 128), F32),
                vmem((n_orb, 8, 128), F32),
                vmem((n_grid, 8, 128), F32),
                dma((n_orb,)), dma((PARTS,)), dma((2,)), dma((2,)),
                dma((n_grid,)), dma((n_grid,)), dma((n_grid,)), dma((n_grid,)),
                dma, dma, dma, dma, dma, dma, dma((PARTS,)), dma((PARTS,)),
                dma((PARTS,)), dma((PARTS,)),
                dma((n_orb,)), dma((n_orb,)), dma((n_grid,)), dma((n_grid,)),
            ],
            compiler_params=pltpu.CompilerParams(
                collective_id=0, has_side_effects=True, vmem_limit_bytes=58 * 1024 * 1024
            ),
        )(orbitals, pivots.reshape(rank, 1))
        return factor, diagonal.reshape(share), peaks[:steps, 0]

    return jax.shard_map(
        on_device,
        mesh=mesh,
        in_specs=(P("orb", "grid"), P()),
        out_specs=(P(("grid", "orb"), None), P(("grid", "orb")), P()),
        check_vma=False,
    )
```

profile of v0, /device:TPU:0, one launch (start us, length us, event | category | flops | bytes accessed | tf_op | source)
XLA Modules:
  0.0 90.7 jit_solution(5025541913469432865)
XLA Ops:
  0.6 1.5 %reshape.14.piv_ref = s32[288,1]{1,0:T(8,128)} reshape(s32[3,96]{1,0:T(4,128)} %param.3) | data formatting | bytes 2304 | tf_op jit(solution)/shard_map/reshape | solution.py:433
  2.1 83.9 %shard_map.49 = (f32[2048,288]{1,0:T(8,128)}, f32[1,2048]{1,0:T(1,128)}, f32[8,128]{1,0:T(8,128)}) custom-call(bf16[450,8192]{1,0:T(8,128)(2,1)} %orb_hbm.1, s32[288,1]{1,0:T(8,128)} %reshape.14.piv_ref), custom_call_target="tpu_custom_call" | custom-call | tf_op jit(solution)/shard_map/pallas_call | solution.py:389
  86.1 0.0 copy-start.1
  86.1 0.0 copy-start
  86.1 3.4 %copy.7 = f32[2048,288]{0,1:T(8,128)} copy(f32[2048,288]{1,0:T(8,128)} %get-tuple-element.12) | data formatting | bytes 4718592
  89.5 0.0 copy-done.1
  89.5 0.6 slice_reduce_fusion
  90.1 0.0 copy-done
  90.1 0.6 copy.9
Async XLA Ops:
  86.1 3.4 %copy-start.1 = (f32[8,128]{1,0:T(8,128)S(1)}, f32[8,128]{1,0:T(8,128)}, u32[]{:S(2)}) copy-start(f32[8,128]{1,0:T(8,128)} %get-tuple-element.8) | copy-start | bytes 12292
  86.1 4.0 %copy-start = (f32[1,2048]{1,0:T(1,128)S(1)}, f32[1,2048]{1,0:T(1,128)}, u32[]{:S(2)}) copy-start(f32[1,2048]{1,0:T(1,128)} %get-tuple-element.7) | copy-start | bytes 24580
where the time goes:
time: 90.9 us; the launch traced here: 90.7 us
  Pallas kernels  83.9 us (92%)
  local copies, waits for them, and re-layouts  6.1 us (7%)
    pallas_call x1, Pallas kernels, on_device(): pl.pallas_call(functools.partial(kernel, n_grid, n_orb, steps, depth * n_...  83.9 us
    unnamed x6, local copies, waits for them, and re-layouts  3.96 us

commit v1 on v0

--- a/solution.py
+++ b/solution.py
@@ -33,14 +33,64 @@
     )
 
 
-def eliminate_small(t, size):
-    row_at = lax.broadcasted_iota(jnp.int32, t.shape, 0)
-    for k in range(size):
-        scale = lax.rsqrt(t[k : k + 1, k : k + 1])
-        row = t[k : k + 1, :] * scale
-        column = t[:, k : k + 1] * scale
-        t = jnp.where(row_at > k, t - column * row, jnp.where(row_at == k, row, t))
-    return t
+def spread_row(t, r):
+    return jnp.broadcast_to(t[r : r + 1, :], (8, 128))
+
+
+def spread_column(t, c):
+    return jnp.broadcast_to(t[:, c : c + 1], (8, 128))
+
+
+def eliminate(square, wide_rows):
+    size = square.shape[0]
+    groups = size // 8
+    width = wide_rows.shape[1] // 128
+    tile = [square[8 * i : 8 * i + 8, :] for i in range(groups)]
+    wide = [
+        [wide_rows[8 * i : 8 * i + 8, 128 * v : 128 * v + 128] for v in range(width)]
+        for i in range(groups)
+    ]
+    row_at = lax.broadcasted_iota(jnp.int32, (8, 128), 0)
+    for j in range(groups):
+        columns = [spread_column(tile[j], 8 * j + c) for c in range(8)]
+        entry = {(r, c): spread_row(columns[c], r) for r in range(8) for c in range(r + 1)}
+        scale, low = [], {}
+        for k in range(8):
+            s = lax.rsqrt(entry[k, k])
+            scale.append(s)
+            for r in range(k + 1, 8):
+                low[r, k] = entry[r, k] * s
+            for r in range(k + 1, 8):
+                for c in range(k + 1, r + 1):
+                    entry[r, c] = entry[r, c] - low[r, k] * low[c, k]
+
+        def forward(rows):
+            done = []
+            for k in range(8):
+                x = rows[k]
+                for c in range(k):
+                    x = x - low[k, c] * done[c]
+                done.append(x * scale[k])
+            return done
+
+        def gather(done):
+            out = done[0]
+            for k in range(1, 8):
+                out = jnp.where(row_at == k, done[k], out)
+            return out
+
+        last = j == groups - 1
+        fresh_tile = None if last else forward([spread_row(tile[j], k) for k in range(8)])
+        fresh_wide = [forward([spread_row(wide[j][v], k) for k in range(8)]) for v in range(width)]
+        for i in range(j + 1, groups):
+            left = forward([spread_column(tile[i], 8 * j + c) for c in range(8)])
+            for k in range(8):
+                tile[i] = tile[i] - left[k] * fresh_tile[k]
+                for v in range(width):
+                    wide[i][v] = wide[i][v] - left[k] * fresh_wide[v][k]
+        for v in range(width):
+            wide[j][v] = gather(fresh_wide[v])
+    return jnp.concatenate([jnp.concatenate(row, axis=1) for row in wide], axis=0)
 
 
 def kernel(
@@ -64,7 +114,6 @@
     rank = slots * slot_rows
     part = share // PARTS
     rows = share * n_orb
-
     loads = []
     for b in range(n_orb):
         copy = pltpu.make_async_copy(
@@ -72,7 +121,6 @@
         )
         copy.start()
         loads.append(copy)
-
     barrier = pltpu.get_barrier_semaphore()
     for d in range(1, n_grid):
         pl.semaphore_signal(
@@ -82,8 +130,52 @@
         pl.semaphore_signal(
             barrier, inc=1, device_id=(g, lax.rem(o + d, n_orb)), device_id_type=MESH
         )
+    base = g * rows
+    flat = jnp.concatenate(
+        [piv_ref[...].astype(F32), jnp.zeros((8 - piv_ref.shape[0], piv_ref.shape[1]), F32)], axis=0
+    ).T
+    wanted = (
+        jnp.concatenate([flat[:, s : s + 1] for s in range(steps)], axis=0).astype(jnp.int32)
+        - base
+    )
+    picked = None
+    for b in range(n_orb):
+        loads[b].wait()
+        lanes = lax.broadcasted_iota(jnp.int32, (rank, share), 1) + b * share
+        hot = jnp.where(lanes == wanted, 1.0, 0.0).astype(BF16)
+        term = dot_nt(hot, own[b])
+        picked = term if picked is None else picked + term
+    picked = picked.astype(BF16)
+    for s in range(slots):
+        mine[s] = picked[s * slot_rows : (s + 1) * slot_rows]
     pl.semaphore_wait(barrier, n_grid + n_orb - 2)
-
+    def first(d):
+        target = lax.rem(g + d, n_grid)
+        return target, pltpu.make_async_remote_copy(
+            src_ref=mine.at[lax.rem(target, slots)],
+            dst_ref=heard.at[d],
+            send_sem=p1_send.at[d],
+            recv_sem=p1_recv.at[d],
+            device_id=(target, o),
+            device_id_type=MESH,
+        )
+
+    def second(d):
+        target = lax.rem(g + d, n_grid)
+        return pltpu.make_async_remote_copy(
+            src_ref=heard.at[0],
+            dst_ref=total.at[lax.rem(g, slots)],
+            send_sem=p2_send.at[d],
+            recv_sem=p2_recv.at[d],
+            device_id=(target, o),
+            device_id_type=MESH,
+        )
+    for d in range(1, n_grid):
+        target, copy = first(d)
+
+        @pl.when(target < slots)
+        def _(copy=copy):
+            copy.start()
     crossing = []
     for yy in range(2):
         start = pl.multiple_of((yy * 2 + 1 - core) * share, share)
@@ -97,49 +189,6 @@
         )
         copy.start()
         crossing.append(copy)
-
-    base = g * rows
-    wanted = piv_ref[...] - base
-    picked = None
-    for b in range(n_orb):
-        loads[b].wait()
-        lanes = lax.broadcasted_iota(jnp.int32, (rank, share), 1) + b * share
-        hot = jnp.where(lanes == wanted, 1.0, 0.0).astype(BF16)
-        term = dot_nt(hot, own[b])
-        picked = term if picked is None else picked + term
-    picked = picked.astype(BF16)
-    for s in range(slots):
-        mine[s] = picked[s * slot_rows : (s + 1) * slot_rows]
-
-    def first(d):
-        target = lax.rem(g + d, n_grid)
-        return target, pltpu.make_async_remote_copy(
-            src_ref=mine.at[lax.rem(target, slots)],
-            dst_ref=heard.at[d],
-            send_sem=p1_send.at[d],
-            recv_sem=p1_recv.at[d],
-            device_id=(target, o),
-            device_id_type=MESH,
-        )
-
-    def second(d):
-        target = lax.rem(g + d, n_grid)
-        return pltpu.make_async_remote_copy(
-            src_ref=heard.at[0],
-            dst_ref=total.at[lax.rem(g, slots)],
-            send_sem=p2_send.at[d],
-            recv_sem=p2_recv.at[d],
-            device_id=(target, o),
-            device_id_type=MESH,
-        )
-
-    for d in range(1, n_grid):
-        target, copy = first(d)
-
-        @pl.when(target < slots)
-        def _(copy=copy):
-            copy.start()
-
     @pl.when(g < slots)
     def _():
         added = mine[lax.rem(g, slots)]
@@ -150,7 +199,6 @@
         for d in range(1, n_grid):
             second(d).start()
         total[lax.rem(g, slots)] = added
-
     for copy in crossing:
         copy.wait_recv()
 
@@ -165,7 +213,6 @@
         )
         point_sum = jnp.sum(a32, axis=0, keepdims=True) + jnp.sum(b32, axis=0, keepdims=True)
         return squares, point_sum
-
     for p in range(PARTS):
         squares, point_sum = moments(across, 1 - side, p)
         side_sums[p] = jnp.zeros((8, part), F32)
@@ -173,14 +220,12 @@
         side_sums[p, 1:2] = point_sum
         squares, _ = moments(o, side, p)
         local[p, rank : rank + 8, :] = jnp.broadcast_to(squares, (8, part))
-
     for d in range(1, n_grid):
         source = lax.rem(g + n_grid - d, n_grid)
 
         @pl.when(source < slots)
         def _(d=d):
             second(d).wait_recv()
-
     swap_copy = pltpu.make_async_remote_copy(
         src_ref=total, dst_ref=swap, send_sem=c_send, recv_sem=c_recv,
         device_id=(g, mate), device_id_type=MESH,
@@ -210,8 +255,6 @@
         a = own[block, :, lo : lo + part]
         b = other[yy, :, lo : lo + part]
         return dot_nn(here, a) + dot_nn(there, b)
-
-
     travel = []
     for p in range(PARTS):
         inner = products(across, 1 - side, p)
@@ -237,7 +280,6 @@
         ):
             copy.start()
             travel.append(copy)
-
     pair_copy.wait_recv()
     half_copy = pltpu.make_async_remote_copy(
         src_ref=pair_recv.at[0], dst_ref=pair_recv.at[1], send_sem=h_send, recv_sem=h_recv,
@@ -257,38 +299,36 @@
         [first_half[:, rank : rank + 1], second_half[:, rank : rank + 1]], axis=0
     )
 
-    def block_step(j, carry):
-        start = pl.multiple_of(j * BLOCK, BLOCK)
-        strip = aug[pl.ds(start, BLOCK), :]
-        pick = jnp.where(
-            lax.broadcasted_iota(jnp.int32, (wide, 128), 0)
-            == lax.broadcasted_iota(jnp.int32, (wide, 128), 1) + start,
-            1.0,
-            0.0,
-        )
-        lane = lax.broadcasted_iota(jnp.int32, (BLOCK, 128), 1)
-        row_at = lax.broadcasted_iota(jnp.int32, (BLOCK, 128), 0)
-        square = dot_nn(strip, pick, HIGHEST)
-        tile = jnp.where(lane < BLOCK, square, jnp.where(lane == row_at + 64, 1.0, 0.0))
-        tile = eliminate_small(tile, BLOCK)
-        inverse = tile[:, 64 : 64 + BLOCK]
+    for j in range(rank // BLOCK):
+        start = j * BLOCK
         at = lax.broadcasted_iota(jnp.int32, (BLOCK, wide), 1)
+        strip = jnp.where(at >= start, aug[start : start + BLOCK, :], 0.0)
+        if j:
+            low_edge = start // 128 * 128
+            high_edge = -(-(start + BLOCK) // 128) * 128
+            done = jnp.concatenate(
+                [
+                    jnp.where(
+                        (at >= start) | (at < i + BLOCK), aug[i : i + BLOCK, :], 0.0
+                    )
+                    for i in range(0, start, BLOCK)
+                ],
+                axis=0,
+            )
+            above = dot_tn(aug[0:start, low_edge:high_edge], done, HIGHEST)
+            strip = strip - above[start - low_edge : start - low_edge + BLOCK, :]
+        square = pltpu.roll(strip, wide - start, 1) if j else strip
+        square = square[:, 0:128]
         unit = jnp.where(at == lax.broadcasted_iota(jnp.int32, (BLOCK, wide), 0) + start, 1.0, 0.0)
-        solved = dot_nn(
-            inverse, jnp.where((at >= start) & (at < start + BLOCK), unit, strip), HIGHEST
-        )
-        multipliers = jnp.where(at >= start + BLOCK, solved, 0.0)
-        every_lane = lax.broadcasted_iota(jnp.int32, (rank, wide), 1)
-        every_row = lax.broadcasted_iota(jnp.int32, (rank, wide), 0)
-        clear = (
-            (every_lane >= start) & (every_lane < start + BLOCK) & (every_row >= start + BLOCK)
-        )
-        aug[...] = jnp.where(clear, 0.0, aug[...]) - dot_tn(multipliers, solved, HIGHEST)[0:rank]
-        aug[pl.ds(start, BLOCK), :] = jnp.where(at < start + BLOCK, solved, 0.0)
-        return carry
-
-    lax.fori_loop(0, rank // BLOCK, block_step, 0)
-    lower_inverse = aug[...]
+        solved = eliminate(square, jnp.where((at >= start) & (at < start + BLOCK), unit, strip))
+        aug[start : start + BLOCK, :] = solved
+    lower_inverse = jnp.concatenate(
+        [
+            jnp.where(at < i + BLOCK, aug[i : i + BLOCK, :], 0.0)
+            for i in range(0, rank, BLOCK)
+        ],
+        axis=0,
+    )
 
     count = rank // steps
     best = [None] * steps
@@ -305,9 +345,9 @@
         columns = jnp.square(inner / orbitals_count)
         diagonal = jnp.square((local[p, rank : rank + 1, :] + far[0:1]) / orbitals_count)
         solved = dot_nn(lower_inverse[:, 0:rank], columns, HIGHEST)
-        out_v[p] = solved.T
+        out_v[p] = solved
         store = pltpu.make_async_copy(
-            out_v.at[p], factor_hbm.at[pl.ds(p * part, part), :], out_sem.at[p]
+            out_v.at[p], factor_hbm.at[:, pl.ds(p * part, part)], out_sem.at[p]
         )
         store.start()
         stores.append(store)
@@ -316,7 +356,6 @@
             diagonal = diagonal - jnp.sum(piece * piece, axis=0, keepdims=True)
             best[s] = diagonal if best[s] is None else jnp.maximum(best[s], diagonal)
         diag_ref[:, p * part : (p + 1) * part] = diagonal
-
     row8 = lax.broadcasted_iota(jnp.int32, (8, 128), 0)
     tile = jnp.zeros((8, 128), F32)
     for s in range(steps):
@@ -349,7 +388,6 @@
         round_grid[d - 1].wait_recv()
         tile = jnp.maximum(tile, tile_grid[d])
     peaks_ref[...] = tile
-
     for store in stores:
         store.wait()
     for d in range(1, n_grid):
@@ -389,7 +427,7 @@
         factor, diagonal, peaks = pl.pallas_call(
             functools.partial(kernel, n_grid, n_orb, steps, depth * n_orb),
             out_shape=(
-                jax.ShapeDtypeStruct((share, rank), F32),
+                jax.ShapeDtypeStruct((rank, share), F32),
                 jax.ShapeDtypeStruct((1, share), F32),
                 jax.ShapeDtypeStruct((8, 128), F32),
             ),
@@ -417,7 +455,7 @@
                 vmem((2, rank // 2, rank + 1), F32),
                 vmem((2, rank // 2, rank + 1), F32),
                 vmem((rank, wide), F32),
-                vmem((PARTS, part, rank), F32),
+                vmem((PARTS, rank, part), F32),
                 vmem((2, 8, 128), F32),
                 vmem((n_orb, 8, 128), F32),
                 vmem((n_grid, 8, 128), F32),
@@ -430,8 +468,8 @@
             compiler_params=pltpu.CompilerParams(
                 collective_id=0, has_side_effects=True, vmem_limit_bytes=58 * 1024 * 1024
             ),
-        )(orbitals, pivots.reshape(rank, 1))
-        return factor, diagonal.reshape(share), peaks[:steps, 0]
+        )(orbitals, pivots)
+        return factor.T, diagonal.reshape(share), peaks[:steps, 0]
 
     return jax.shard_map(
         on_device,

time: 90.9 us -> 76.9 us (0.85)
  Pallas kernels: 83.9 us -> 70.8 us
    pallas_call x1, Pallas kernels: 83.9 us -> 70.8 us  [on_device(): pl.pallas_call(functools.partial(kernel, n_grid, n_orb, steps, depth * n_...]
    reshape x1 -> x0, local copies, waits for them, and re-layouts: 1.52 us -> none  [on_device(): pivots.reshape(rank, 1)]
    unnamed x6 -> x4, local copies, waits for them, and re-layouts: 3.96 us -> 3.94 us
where the time goes in v1:
time: 76.9 us; the launch traced here: 76.7 us
  Pallas kernels  70.8 us (92%)
  local copies, waits for them, and re-layouts  5.24 us (7%)
    pallas_call x1, Pallas kernels, on_device(): pl.pallas_call(functools.partial(kernel, n_grid, n_orb, steps, depth * n_...  70.8 us
    unnamed x4, local copies, waits for them, and re-layouts  3.94 us

profile of v1, /device:TPU:0, one launch (start us, length us, event | category | flops | bytes accessed | tf_op | source)
XLA Modules:
  0.0 76.7 jit_solution(5345165629850491726)
XLA Ops:
  0.6 70.8 %shard_map.49 = (f32[288,2048]{1,0:T(8,128)}, f32[1,2048]{1,0:T(1,128)}, f32[8,128]{1,0:T(8,128)}) custom-call(bf16[450,8192]{1,0:T(8,128)(2,1)} %orb_hbm.1, s32[3,96]{1,0:T(4,128)} %piv_ref.1), custom_call_target="tpu_custom_call" | custom-call | tf_op jit(solution)/shard_map/pallas_call | solution.py:427
  71.4 1.3 %slice_reduce_fusion = f32[3]{0:T(128)} fusion(f32[8,128]{1,0:T(8,128)} %get-tuple-element.8), kind=kLoop, calls=%fused_computation | loop fusion | bytes 24 | tf_op jit(solution)/shard_map/slice | solution.py:472
  72.7 0.0 copy-start
  72.7 3.3 %copy.7 = f32[2048,288]{0,1:T(8,128)} copy(f32[2048,288]{0,1:T(8,128)} %bitcast.2) | data formatting | bytes 4718592
  76.1 0.0 copy-done
  76.1 0.6 copy.8
Async XLA Ops:
  72.7 3.3 %copy-start = (f32[1,2048]{1,0:T(1,128)S(1)}, f32[1,2048]{1,0:T(1,128)}, u32[]{:S(2)}) copy-start(f32[1,2048]{1,0:T(1,128)} %get-tuple-element.7) | copy-start | bytes 24580

commit v2 on v1

v2 whole, which is shorter than its diff:
```python
import functools

import jax
import jax.numpy as jnp
from jax import lax
from jax.experimental import pallas as pl
from jax.experimental.pallas import tpu as pltpu
from jax.sharding import PartitionSpec as P

F32 = jnp.float32
BF16 = jnp.bfloat16
HIGHEST = lax.Precision.HIGHEST
MESH = pl.DeviceIdType.MESH
BLOCK = 48
AHEAD = 2


def dot_nn(a, b, precision=None):
    return lax.dot_general(
        a, b, (((1,), (0,)), ((), ())), precision=precision, preferred_element_type=F32
    )


def dot_nt(a, b, precision=None):
    return lax.dot_general(
        a, b, (((1,), (1,)), ((), ())), precision=precision, preferred_element_type=F32
    )


def dot_tn(a, b, precision=None):
    return lax.dot_general(
        a, b, (((0,), (0,)), ((), ())), precision=precision, preferred_element_type=F32
    )


def spread_row(t, r):
    return jnp.broadcast_to(t[r : r + 1, :], (8, 128))


def spread_column(t, c):
    return jnp.broadcast_to(t[:, c : c + 1], (8, 128))


def eliminate(square, wide_rows):
    size = square.shape[0]
    groups = size // 8
    width = wide_rows.shape[1] // 128
    tile = [square[8 * i : 8 * i + 8, :] for i in range(groups)]
    wide = [
        [wide_rows[8 * i : 8 * i + 8, 128 * v : 128 * v + 128] for v in range(width)]
        for i in range(groups)
    ]
    row_at = lax.broadcasted_iota(jnp.int32, (8, 128), 0)
    for j in range(groups):
        columns = [spread_column(tile[j], 8 * j + c) for c in range(8)]
        entry = {(r, c): spread_row(columns[c], r) for r in range(8) for c in range(r + 1)}
        scale, low = [], {}
        for k in range(8):
            s = lax.rsqrt(entry[k, k])
            scale.append(s)
            for r in range(k + 1, 8):
                low[r, k] = entry[r, k] * s
            for r in range(k + 1, 8):
                for c in range(k + 1, r + 1):
                    entry[r, c] = entry[r, c] - low[r, k] * low[c, k]

        def forward(rows):
            done = []
            for k in range(8):
                x = rows[k]
                for c in range(k):
                    x = x - low[k, c] * done[c]
                done.append(x * scale[k])
            return done

        def gather(done):
            out = done[0]
            for k in range(1, 8):
                out = jnp.where(row_at == k, done[k], out)
            return out

        last = j == groups - 1
        fresh_tile = None if last else forward([spread_row(tile[j], k) for k in range(8)])
        fresh_wide = [forward([spread_row(wide[j][v], k) for k in range(8)]) for v in range(width)]
        for i in range(j + 1, groups):
            left = forward([spread_column(tile[i], 8 * j + c) for c in range(8)])
            for k in range(8):
                tile[i] = tile[i] - left[k] * fresh_tile[k]
                for v in range(width):
                    wide[i][v] = wide[i][v] - left[k] * fresh_wide[v][k]
        for v in range(width):
            wide[j][v] = gather(fresh_wide[v])
    return jnp.concatenate([jnp.concatenate(row, axis=1) for row in wide], axis=0)


def layout(rank, count, depth, n_grid):
    groups = [(0, count), (count, rank - count)] if rank > count else [(0, rank)]
    tiles = -(-depth // 128)
    cuts = []
    for _, rows in groups:
        parts = max(
            (r for r in range(1, rows // 16 + 1) if r * tiles <= n_grid and rows % (16 * r) == 0),
            default=1,
        )
        cuts.append((parts, rows // parts))
    return groups, tiles, cuts


def pieces_of(share):
    units = share // 128
    sizes = [units * 5 // 16, units * 5 // 16, units * 4 // 16]
    sizes.append(units - sum(sizes))
    starts = [sum(sizes[:i]) for i in range(len(sizes))]
    return [(128 * a, 128 * n) for a, n in zip(starts, sizes) if n]


def kernel(
    n_grid, n_orb, steps, orbitals_count, plan,
    orb_hbm, piv_hbm,
    factor_hbm, diag_ref, peaks_ref,
    piv_ref, own, other, mines, totals, heards, swaps, sums, arrived, scales, far_scales,
    moment, far_moment, local, own_squares, pair_send, pair_recv,
    aug, out_v, tile_mine, tile_orb, tile_grid,
    piv_sem, load_sem, out_sem, x_send, x_recv, p1_send, p1_recv, p2_send, p2_recv,
    c_send, c_recv, q_send, q_recv, h_send, h_recv, s_send, s_recv, z_send, z_recv,
    m_send, m_recv, mo_send, mo_recv, mg_send, mg_recv,
):
    groups, tiles, cuts = plan
    g = lax.axis_index("grid")
    o = lax.axis_index("orb")
    core = lax.rem(o, 2)
    side = o // 2
    mate = o + 1 - 2 * core
    across = (1 - side) * 2 + core
    depth, share = own.shape[1], own.shape[2]
    count = piv_ref.shape[1]
    rank = steps * count
    rows = share * n_orb
    pieces = pieces_of(share)
    n_groups = len(groups)
    piv_copy = pltpu.make_async_copy(piv_hbm, piv_ref, piv_sem)
    piv_copy.start()
    loads = []
    for b in range(n_orb):
        copy = pltpu.make_async_copy(
            orb_hbm.at[:, pl.ds(b * share, share)], own.at[b], load_sem.at[b]
        )
        copy.start()
        loads.append(copy)

    barrier = pltpu.get_barrier_semaphore()
    for d in range(1, n_grid):
        pl.semaphore_signal(
            barrier, inc=1, device_id=(lax.rem(g + d, n_grid), o), device_id_type=MESH
        )
    for d in range(1, n_orb):
        pl.semaphore_signal(
            barrier, inc=1, device_id=(g, lax.rem(o + d, n_orb)), device_id_type=MESH
        )
    piv_copy.wait()
    base = g * rows
    flat = jnp.concatenate(
        [piv_ref[...].astype(F32), jnp.zeros((8 - piv_ref.shape[0], count), F32)], axis=0
    ).T
    wanted = (
        jnp.concatenate([flat[:, s : s + 1] for s in range(steps)], axis=0).astype(jnp.int32)
        - base
    )
    picked = None
    for b in range(n_orb):
        loads[b].wait()
        lanes = lax.broadcasted_iota(jnp.int32, (rank, share), 1) + b * share
        hot = jnp.where(lanes == wanted, 1.0, 0.0).astype(BF16)
        term = dot_nt(hot, own[b])
        picked = term if picked is None else picked + term
    picked = jnp.concatenate(
        [picked.astype(BF16), jnp.zeros((rank, tiles * 128 - depth), BF16)], axis=1
    )
    for i, (first_row, _) in enumerate(groups):
        parts, size = cuts[i]
        for q in range(parts * tiles):
            at = first_row + q // tiles * size
            lane = q % tiles * 128
            mines[i][q] = picked[at : at + size, lane : lane + 128]
    pl.semaphore_wait(barrier, n_grid + n_orb - 2)

    def block_of(i, owner):
        return lax.rem(owner, cuts[i][0] * tiles)

    def owned(i, owner, action):
        if cuts[i][0] * tiles == n_grid:
            action()
        else:
            pl.when(owner < cuts[i][0] * tiles)(action)

    def first(i, d):
        target = lax.rem(g + d, n_grid)
        return target, pltpu.make_async_remote_copy(
            src_ref=mines[i].at[block_of(i, target)],
            dst_ref=heards[i].at[d],
            send_sem=p1_send.at[i, d],
            recv_sem=p1_recv.at[i, d],
            device_id=(target, o),
            device_id_type=MESH,
        )

    def second(i, d):
        target = lax.rem(g + d, n_grid)
        return pltpu.make_async_remote_copy(
            src_ref=heards[i].at[0],
            dst_ref=totals[i].at[block_of(i, g)],
            send_sem=p2_send.at[i, d],
            recv_sem=p2_recv.at[i, d],
            device_id=(target, o),
            device_id_type=MESH,
        )
    for i in range(n_groups):
        for d in range(1, n_grid):
            target, copy = first(i, d)
            owned(i, target, copy.start)

    crossing = []
    for yy in range(2):
        start = pl.multiple_of((yy * 2 + 1 - core) * share, share)
        copy = pltpu.make_async_remote_copy(
            src_ref=orb_hbm.at[:, pl.ds(start, share)],
            dst_ref=other.at[yy],
            send_sem=x_send.at[yy],
            recv_sem=x_recv.at[yy],
            device_id=(g, mate),
            device_id_type=MESH,
        )
        copy.start()
        crossing.append(copy)

    for i in range(n_groups):

        def add_up(i=i):
            added = mines[i][block_of(i, g)]
            for d in range(1, n_grid):
                first(i, d)[1].wait_recv()
                added = added + heards[i][d]
            heards[i][0] = added
            for d in range(1, n_grid):
                second(i, d).start()
            totals[i][block_of(i, g)] = added

        owned(i, g, add_up)
    for copy in crossing:
        copy.wait_recv()

    def squares_of(block):
        x = block.astype(F32)
        return jnp.sum(x * x, axis=0, keepdims=True)

    def sum_of(block):
        return jnp.sum(block.astype(F32), axis=0, keepdims=True)

    for lo, n in pieces:
        a, b = own[across, :, lo : lo + n], other[1 - side, :, lo : lo + n]
        moment[:, lo : lo + n] = squares_of(a) + squares_of(b)
        moment[:, share + lo : share + lo + n] = sum_of(a) + sum_of(b)
    moment_copy = pltpu.make_async_remote_copy(
        src_ref=moment, dst_ref=far_moment, send_sem=m_send, recv_sem=m_recv,
        device_id=(g, across), device_id_type=MESH,
    )
    moment_copy.start()

    def gathered(i, ref):
        parts, _ = cuts[i]
        return jnp.concatenate(
            [
                jnp.concatenate([ref[r * tiles + t] for t in range(tiles)], axis=1)
                for r in range(parts)
            ],
            axis=0,
        )[:, 0:depth]

    swapping, here, there, means = [], [], [], []

    def meet(i):
        for d in range(1, n_grid):
            source = lax.rem(g + n_grid - d, n_grid)
            owned(i, source, second(i, d).wait_recv)
        copy = pltpu.make_async_remote_copy(
            src_ref=totals[i], dst_ref=swaps[i], send_sem=c_send.at[i], recv_sem=c_recv.at[i],
            device_id=(g, mate), device_id_type=MESH,
        )
        copy.start()
        swapping.append(copy)
        here.append(gathered(i, totals[i]))
        copy.wait_recv()
        there.append(gathered(i, swaps[i]))
        means.append(
            (
                jnp.sum(here[i].astype(F32), axis=1, keepdims=True)
                + jnp.sum(there[i].astype(F32), axis=1, keepdims=True)
            )
            / (2.0 * depth)
        )

    travel = {}

    def code(i, p):
        lo, n = pieces[p]
        top, size = groups[i]
        inner = dot_nn(here[i], own[across, :, lo : lo + n]) + dot_nn(
            there[i], other[1 - side, :, lo : lo + n]
        )
        rest = inner - means[i] * moment[:, share + lo : share + lo + n]
        most = jnp.max(jnp.abs(rest), axis=0, keepdims=True)
        step = jnp.maximum(most * (1.0 / 32767.0), 1e-30)
        coded = jnp.clip(jnp.round(rest * (1.0 / step)), -32767.0, 32767.0)
        sums[top : top + size, lo : lo + n] = coded.astype(jnp.int32).astype(jnp.int16)
        scales[:, i * share + lo : i * share + lo + n] = step

    def send(i, p):
        lo, n = pieces[p]
        top, size = groups[i]
        travel[i, p] = (
            pltpu.make_async_remote_copy(
                src_ref=scales.at[:, pl.ds(i * share + lo, n)],
                dst_ref=far_scales.at[:, pl.ds(i * share + lo, n)],
                send_sem=z_send.at[i, p], recv_sem=z_recv.at[i, p],
                device_id=(g, across), device_id_type=MESH,
            ),
            pltpu.make_async_remote_copy(
                src_ref=sums.at[pl.ds(top, size), pl.ds(lo, n)],
                dst_ref=arrived.at[pl.ds(top, size), pl.ds(lo, n)],
                send_sem=s_send.at[i, p], recv_sem=s_recv.at[i, p],
                device_id=(g, across), device_id_type=MESH,
            ),
        )
        for copy in travel[i, p]:
            copy.start()

    late = n_groups - 1
    for i in range(late):
        meet(i)
        for p in range(len(pieces)):
            code(i, p)
            if i or p < AHEAD:
                send(i, p)
    meet(late)
    here_all = jnp.concatenate(here, axis=0)
    there_all = jnp.concatenate(there, axis=0)
    mean_all = jnp.concatenate(means, axis=0)
    pair = dot_nt(here_all, here_all) + dot_nt(there_all, there_all)
    corners = [(r, c) for r in range(steps) for c in range(r, steps)]
    half = len(corners) // 2

    def corner(r, c):
        return pair[r * count : (r + 1) * count, c * count : (c + 1) * count]

    for k, (r, c) in enumerate(corners):
        pair_send[k // half, k % half, :, 0:count] = corner(r, c)
        pair_send[k // half, k % half, :, count : count + 1] = mean_all[
            r * count : (r + 1) * count
        ]
    pair_copy = pltpu.make_async_remote_copy(
        src_ref=pair_send.at[core], dst_ref=pair_recv.at[0], send_sem=q_send, recv_sem=q_recv,
        device_id=(g, across), device_id_type=MESH,
    )
    pair_copy.start()
    if late:
        for p in range(AHEAD, len(pieces)):
            send(0, p)
    for p in range(len(pieces)):
        code(late, p)
        send(late, p)
    for lo, n in pieces:
        a, b = own[o, :, lo : lo + n], other[side, :, lo : lo + n]
        local[:, lo : lo + n] = dot_nn(here_all, a) + dot_nn(there_all, b)
        own_squares[:, lo : lo + n] = squares_of(a) + squares_of(b)
    pair_copy.wait_recv()
    half_copy = pltpu.make_async_remote_copy(
        src_ref=pair_recv.at[0], dst_ref=pair_recv.at[1], send_sem=h_send, recv_sem=h_recv,
        device_id=(g, mate), device_id_type=MESH,
    )
    half_copy.start()
    half_copy.wait_recv()
    wide = aug.shape[1]
    aug[...] = jnp.zeros((rank, wide), F32)
    far_means = [None] * steps
    for k, (r, c) in enumerate(corners):
        which = core if k < half else 1 - core
        far = pair_recv[which, k % half]
        aug[r * count : (r + 1) * count, 128 * c : 128 * c + count] = jnp.square(
            (pair_send[k // half, k % half] + far)[:, 0:count] / orbitals_count
        )
        far_means[r] = far[:, count : count + 1]
    far_mean = jnp.concatenate(far_means, axis=0)

    def lane_of(row):
        return row // count * 128 + row % count

    at = lax.broadcasted_iota(jnp.int32, (BLOCK, wide), 1)
    eye_row = lax.broadcasted_iota(jnp.int32, (BLOCK, wide), 0)
    for start in range(0, rank, BLOCK):
        lane = lane_of(start)
        tile = lane // 128 * 128
        strip = jnp.where(at >= lane, aug[start : start + BLOCK, :], 0.0)
        if start:
            done = jnp.concatenate(
                [
                    jnp.where(
                        (at >= lane) | (at < lane_of(i) + BLOCK), aug[i : i + BLOCK, :], 0.0
                    )
                    for i in range(0, start, BLOCK)
                ],
                axis=0,
            )
            above = dot_tn(aug[0:start, tile : tile + 128], done, HIGHEST)
            strip = strip - above[lane - tile : lane - tile + BLOCK, :]
        square = strip[:, tile : tile + 128]
        if lane > tile:
            square = pltpu.roll(square, 128 - (lane - tile), 1)
        unit = jnp.where(at == eye_row + lane, 1.0, 0.0)
        aug[start : start + BLOCK, :] = eliminate(
            square, jnp.where((at >= lane) & (at < lane + BLOCK), unit, strip)
        )
    inverse = []
    for s in range(steps):
        bands = []
        for i in range(s * count, (s + 1) * count, BLOCK):
            bands.append(jnp.where(at < lane_of(i) + BLOCK, aug[i : i + BLOCK, :], 0.0))
        band = jnp.concatenate(bands, axis=0)
        inverse.append(
            jnp.concatenate([band[:, 128 * c : 128 * c + count] for c in range(s + 1)], axis=1)
        )

    best = [None] * steps
    stores = []
    moment_copy.wait_recv()
    for p, (lo, n) in enumerate(pieces):
        for i in range(n_groups):
            for copy in travel[i, p]:
                copy.wait_recv()
        scale = jnp.concatenate(
            [
                jnp.broadcast_to(
                    far_scales[:, i * share + lo : i * share + lo + n], (size, n)
                )
                for i, (_, size) in enumerate(groups)
            ],
            axis=0,
        )
        inner = (
            local[:, lo : lo + n]
            + arrived[:, lo : lo + n].astype(jnp.int32).astype(F32) * scale
            + far_mean * far_moment[:, share + lo : share + lo + n]
        )
        columns = jnp.square(inner / orbitals_count)
        diagonal = jnp.square(
            (own_squares[:, lo : lo + n] + far_moment[:, lo : lo + n]) / orbitals_count
        )
        for s in range(steps):
            solved = dot_nn(inverse[s], columns[0 : (s + 1) * count], HIGHEST)
            out_v[s * count : (s + 1) * count, lo : lo + n] = solved
            diagonal = diagonal - jnp.sum(solved * solved, axis=0, keepdims=True)
            top = jnp.max(diagonal, axis=1, keepdims=True)
            best[s] = top if best[s] is None else jnp.maximum(best[s], top)
        store = pltpu.make_async_copy(
            out_v.at[:, pl.ds(lo, n)], factor_hbm.at[:, pl.ds(lo, n)], out_sem.at[p]
        )
        store.start()
        stores.append(store)
        diag_ref[:, lo : lo + n] = diagonal
    row8 = lax.broadcasted_iota(jnp.int32, (8, 128), 0)
    tile = jnp.zeros((8, 128), F32)
    for s in range(steps):
        tile = jnp.where(row8 == s, jnp.broadcast_to(best[s], (8, 128)), tile)
    tile_mine[0] = tile
    round_orb = []
    for d in range(1, n_orb):
        copy = pltpu.make_async_remote_copy(
            src_ref=tile_mine.at[0], dst_ref=tile_orb.at[d],
            send_sem=mo_send.at[d], recv_sem=mo_recv.at[d],
            device_id=(g, lax.rem(o + d, n_orb)), device_id_type=MESH,
        )
        copy.start()
        round_orb.append(copy)
    for d in range(1, n_orb):
        round_orb[d - 1].wait_recv()
        tile = jnp.maximum(tile, tile_orb[d])
    tile_mine[1] = tile
    round_grid = []
    for d in range(1, n_grid):
        copy = pltpu.make_async_remote_copy(
            src_ref=tile_mine.at[1], dst_ref=tile_grid.at[d],
            send_sem=mg_send.at[d], recv_sem=mg_recv.at[d],
            device_id=(lax.rem(g + d, n_grid), o), device_id_type=MESH,
        )
        copy.start()
        round_grid.append(copy)
    for d in range(1, n_grid):
        round_grid[d - 1].wait_recv()
        tile = jnp.maximum(tile, tile_grid[d])
    peaks_ref[...] = tile
    for store in stores:
        store.wait()
    for i in range(n_groups):
        for d in range(1, n_grid):
            target, copy = first(i, d)
            owned(i, target, copy.wait_send)

        def sent(i=i):
            for d in range(1, n_grid):
                second(i, d).wait_send()

        owned(i, g, sent)

    for copy in crossing + swapping + [moment_copy, pair_copy, half_copy] + round_orb + round_grid:
        copy.wait_send()
    for pair_of in travel.values():
        for copy in pair_of:
            copy.wait_send()


def solution(mesh):
    n_grid, n_orb = mesh.shape["grid"], mesh.shape["orb"]
    assert n_orb == 4

    def on_device(orbitals, pivots):
        depth, rows = orbitals.shape
        steps, count = pivots.shape
        rank = steps * count
        share = rows // n_orb
        plan = layout(rank, count, depth, n_grid)
        groups, tiles, cuts = plan
        n_groups = len(groups)
        n_pieces = len(pieces_of(share))
        wide = steps * 128
        corners = steps * (steps + 1) // 2
        assert count < 128 and count % BLOCK == 0 and corners % 2 == 0
        dma = pltpu.SemaphoreType.DMA
        vmem = pltpu.VMEM
        blocks = [vmem((r * tiles, size, 128), BF16) for r, size in cuts]
        factor, diagonal, peaks = pl.pallas_call(
            functools.partial(kernel, n_grid, n_orb, steps, depth * n_orb, plan),
            out_shape=(
                jax.ShapeDtypeStruct((rank, share), F32),
                jax.ShapeDtypeStruct((1, share), F32),
                jax.ShapeDtypeStruct((8, 128), F32),
            ),
            in_specs=[
                pl.BlockSpec(memory_space=pltpu.HBM),
                pl.BlockSpec(memory_space=pltpu.HBM),
            ],
            out_specs=(
                pl.BlockSpec(memory_space=pl.ANY),
                pl.BlockSpec(memory_space=vmem),
                pl.BlockSpec(memory_space=vmem),
            ),
            scratch_shapes=[
                vmem((steps, count), jnp.int32),
                vmem((n_orb, depth, share), BF16),
                vmem((2, depth, share), BF16),
                blocks,
                blocks,
                [vmem((n_grid, size, 128), BF16) for _, size in cuts],
                blocks,
                vmem((rank, share), jnp.int16),
                vmem((rank, share), jnp.int16),
                vmem((1, n_groups * share), F32),
                vmem((1, n_groups * share), F32),
                vmem((1, 2 * share), F32),
                vmem((1, 2 * share), F32),
                vmem((rank, share), F32),
                vmem((1, share), F32),
                vmem((2, corners // 2, count, 128), F32),
                vmem((2, corners // 2, count, 128), F32),
                vmem((rank, wide), F32),
                vmem((rank, share), F32),
                vmem((2, 8, 128), F32),
                vmem((n_orb, 8, 128), F32),
                vmem((n_grid, 8, 128), F32),
                dma, dma((n_orb,)), dma((n_pieces,)), dma((2,)), dma((2,)),
                dma((n_groups, n_grid)), dma((n_groups, n_grid)),
                dma((n_groups, n_grid)), dma((n_groups, n_grid)),
                dma((n_groups,)), dma((n_groups,)), dma, dma, dma, dma,
                dma((n_groups, n_pieces)), dma((n_groups, n_pieces)),
                dma((n_groups, n_pieces)), dma((n_groups, n_pieces)),
                dma, dma,
                dma((n_orb,)), dma((n_orb,)), dma((n_grid,)), dma((n_grid,)),
            ],
            compiler_params=pltpu.CompilerParams(
                collective_id=0, has_side_effects=True, vmem_limit_bytes=46 * 1024 * 1024
            ),
        )(
            pltpu.with_memory_space_constraint(orbitals, pltpu.HBM),
            pltpu.with_memory_space_constraint(pivots, pltpu.HBM),
        )
        return factor.T, diagonal.reshape(share), peaks[:steps, 0]

    return jax.shard_map(
        on_device,
        mesh=mesh,
        in_specs=(P("orb", "grid"), P()),
        out_specs=(P(("grid", "orb"), None), P(("grid", "orb")), P()),
        check_vma=False,
    )
```

time: 76.9 us -> 63.9 us (0.83)
  Pallas kernels: 70.8 us -> 60.5 us
  local copies, waits for them, and re-layouts: 5.24 us -> 2.63 us
    pallas_call x1, Pallas kernels: 70.8 us -> 60.5 us  [on_device(): pl.pallas_call(functools.partial(kernel, n_grid, n_orb, steps, depth * n_...]
    unnamed x4 -> x2, local copies, waits for them, and re-layouts: 3.94 us -> 2 us
where the time goes in v2:
time: 63.9 us; the launch traced here: 63.8 us
  Pallas kernels  60.5 us (95%)
  local copies, waits for them, and re-layouts  2.63 us (4%)
  between operations  0.64 us (1%)
    pallas_call x1, Pallas kernels, on_device(): pl.pallas_call(functools.partial(kernel, n_grid, n_orb, steps, depth * n_...  60.5 us
    unnamed x2, local copies, waits for them, and re-layouts  2 us

profile of v2, /device:TPU:0, one launch (start us, length us, event | category | flops | bytes accessed | tf_op | source)
XLA Modules:
  0.0 63.8 jit_solution(4020568909508828058)
XLA Ops:
  0.6 60.5 %shard_map.49 = (f32[288,2048]{1,0:T(8,128)S(1)}, f32[1,2048]{1,0:T(1,128)S(1)}, f32[8,128]{1,0:T(8,128)S(1)}) custom-call(bf16[450,8192]{1,0:T(8,128)(2,1)} %orb_hbm.1, s32[3,96]{1,0:T(4,128)} %piv_hbm.1), custom_call_target="tpu_custom_call" | custom-call | tf_op jit(solution)/shard_map/pallas_call | solution.py:539
  61.1 0.6 slice_reduce_fusion
  61.7 1.4 %copy.7 = f32[2048,288]{0,1:T(8,128)} copy(f32[2048,288]{0,1:T(8,128)S(1)} %bitcast.2) | data formatting | bytes 4718592
  63.2 0.6 copy.8

commit v3 on v2

--- a/solution.py
+++ b/solution.py
@@ -12,7 +12,8 @@
 HIGHEST = lax.Precision.HIGHEST
 MESH = pl.DeviceIdType.MESH
 BLOCK = 48
-AHEAD = 2
+AHEAD = 3
+ONE_ROUND = 32
 
 
 def dot_nn(a, b, precision=None):
@@ -94,7 +95,7 @@
 
 
 def layout(rank, count, depth, n_grid):
-    groups = [(0, count), (count, rank - count)] if rank > count else [(0, rank)]
+    groups = [(top, count) for top in range(0, rank, count)]
     tiles = -(-depth // 128)
     cuts = []
     for _, rows in groups:
@@ -119,11 +120,11 @@
     orb_hbm, piv_hbm,
     factor_hbm, diag_ref, peaks_ref,
     piv_ref, own, other, mines, totals, heards, swaps, sums, arrived, scales, far_scales,
-    moment, far_moment, local, own_squares, pair_send, pair_recv,
-    aug, out_v, tile_mine, tile_orb, tile_grid,
+    moment, far_moment, local, own_squares, pair_sends, pair_recvs,
+    aug, out_v, tile_mine, tile_far,
     piv_sem, load_sem, out_sem, x_send, x_recv, p1_send, p1_recv, p2_send, p2_recv,
     c_send, c_recv, q_send, q_recv, h_send, h_recv, s_send, s_recv, z_send, z_recv,
-    m_send, m_recv, mo_send, mo_recv, mg_send, mg_recv,
+    m_send, m_recv, mo_send, mo_recv,
 ):
     groups, tiles, cuts = plan
     g = lax.axis_index("grid")
@@ -140,24 +141,41 @@
     n_groups = len(groups)
     piv_copy = pltpu.make_async_copy(piv_hbm, piv_ref, piv_sem)
     piv_copy.start()
-    loads = []
-    for b in range(n_orb):
-        copy = pltpu.make_async_copy(
+    loads = [
+        pltpu.make_async_copy(
             orb_hbm.at[:, pl.ds(b * share, share)], own.at[b], load_sem.at[b]
         )
+        for b in range(n_orb)
+    ]
+    loads[0].start()
+
+    def partner(d):
+        if n_grid & (n_grid - 1):
+            return lax.rem(n_grid + d - g, n_grid)
+        at = g
+        for bit in range(n_grid.bit_length() - 1):
+            if d >> bit & 1:
+                at = at + (1 - 2 * lax.rem(g // (1 << bit), 2)) * (1 << bit)
+        return at
+
+    reach = [
+        (dg, do)
+        for dg in range(n_grid - 1, -1, -1)
+        for do in range(n_orb - 1, -1, -1)
+        if (dg or do) and (ONE_ROUND >= n_grid * n_orb or not (dg and do))
+    ]
+
+    def far_device(dg, do):
+        return (partner(dg) if dg else g, lax.rem(o + do, n_orb) if do else o)
+
+    barrier = pltpu.get_barrier_semaphore()
+    for dg, do in reach:
+        pl.semaphore_signal(
+            barrier, inc=1, device_id=far_device(dg, do), device_id_type=MESH
+        )
+    piv_copy.wait()
+    for copy in loads[1:]:
         copy.start()
-        loads.append(copy)
-
-    barrier = pltpu.get_barrier_semaphore()
-    for d in range(1, n_grid):
-        pl.semaphore_signal(
-            barrier, inc=1, device_id=(lax.rem(g + d, n_grid), o), device_id_type=MESH
-        )
-    for d in range(1, n_orb):
-        pl.semaphore_signal(
-            barrier, inc=1, device_id=(g, lax.rem(o + d, n_orb)), device_id_type=MESH
-        )
-    piv_copy.wait()
     base = g * rows
     flat = jnp.concatenate(
         [piv_ref[...].astype(F32), jnp.zeros((8 - piv_ref.shape[0], count), F32)], axis=0
@@ -182,7 +200,7 @@
             at = first_row + q // tiles * size
             lane = q % tiles * 128
             mines[i][q] = picked[at : at + size, lane : lane + 128]
-    pl.semaphore_wait(barrier, n_grid + n_orb - 2)
+    pl.semaphore_wait(barrier, len(reach))
 
     def block_of(i, owner):
         return lax.rem(owner, cuts[i][0] * tiles)
@@ -193,8 +211,10 @@
         else:
             pl.when(owner < cuts[i][0] * tiles)(action)
 
+    others = range(n_grid - 1, 0, -1)
+
     def first(i, d):
-        target = lax.rem(g + d, n_grid)
+        target = partner(d)
         return target, pltpu.make_async_remote_copy(
             src_ref=mines[i].at[block_of(i, target)],
             dst_ref=heards[i].at[d],
@@ -205,7 +225,7 @@
         )
 
     def second(i, d):
-        target = lax.rem(g + d, n_grid)
+        target = partner(d)
         return pltpu.make_async_remote_copy(
             src_ref=heards[i].at[0],
             dst_ref=totals[i].at[block_of(i, g)],
@@ -214,10 +234,13 @@
             device_id=(target, o),
             device_id_type=MESH,
         )
-    for i in range(n_groups):
-        for d in range(1, n_grid):
+    def scatter(i):
+        for d in others:
             target, copy = first(i, d)
             owned(i, target, copy.start)
+
+    for i in range(min(2, n_groups)):
+        scatter(i)
 
     crossing = []
     for yy in range(2):
@@ -233,19 +256,24 @@
         copy.start()
         crossing.append(copy)
 
-    for i in range(n_groups):
-
-        def add_up(i=i):
+    def add_up(i):
+
+        def action():
             added = mines[i][block_of(i, g)]
-            for d in range(1, n_grid):
+            for d in reversed(others):
                 first(i, d)[1].wait_recv()
                 added = added + heards[i][d]
             heards[i][0] = added
-            for d in range(1, n_grid):
+            for d in others:
                 second(i, d).start()
             totals[i][block_of(i, g)] = added
 
-        owned(i, g, add_up)
+        owned(i, g, action)
+        if i + 2 < n_groups:
+            scatter(i + 2)
+
+    for i in range(min(2, n_groups)):
+        add_up(i)
     for copy in crossing:
         copy.wait_recv()
 
@@ -276,12 +304,12 @@
             axis=0,
         )[:, 0:depth]
 
-    swapping, here, there, means = [], [], [], []
+    swapping, here, there, means, pair_copies = [], [], [], [], []
+    half = count // 2
 
     def meet(i):
-        for d in range(1, n_grid):
-            source = lax.rem(g + n_grid - d, n_grid)
-            owned(i, source, second(i, d).wait_recv)
+        for d in reversed(others):
+            owned(i, partner(d), second(i, d).wait_recv)
         copy = pltpu.make_async_remote_copy(
             src_ref=totals[i], dst_ref=swaps[i], send_sem=c_send.at[i], recv_sem=c_recv.at[i],
             device_id=(g, mate), device_id_type=MESH,
@@ -289,6 +317,11 @@
         copy.start()
         swapping.append(copy)
         here.append(gathered(i, totals[i]))
+        if i == 0:
+            lo, n = pieces[0]
+            out_v[0 : groups[0][1], lo : lo + n] = dot_nn(here[0], own[across, :, lo : lo + n])
+        if i + 2 < n_groups:
+            add_up(i + 2)
         copy.wait_recv()
         there.append(gathered(i, swaps[i]))
         means.append(
@@ -298,15 +331,34 @@
             )
             / (2.0 * depth)
         )
+        pair = dot_nt(jnp.concatenate(here, axis=0), here[i]) + dot_nt(
+            jnp.concatenate(there, axis=0), there[i]
+        )
+        for h in range(2):
+            for r in range(i + 1):
+                top = r * count + h * half
+                pair_sends[i][h, r * half : (r + 1) * half, 0:count] = pair[top : top + half]
+            pair_sends[i][h, i * half : (i + 1) * half, count : count + 1] = means[i][
+                h * half : (h + 1) * half
+            ]
+        pair_copy = pltpu.make_async_remote_copy(
+            src_ref=pair_sends[i].at[core], dst_ref=pair_recvs[i].at[0],
+            send_sem=q_send.at[i], recv_sem=q_recv.at[i],
+            device_id=(g, across), device_id_type=MESH,
+        )
+        pair_copy.start()
+        pair_copies.append(pair_copy)
 
     travel = {}
 
     def code(i, p):
         lo, n = pieces[p]
         top, size = groups[i]
-        inner = dot_nn(here[i], own[across, :, lo : lo + n]) + dot_nn(
-            there[i], other[1 - side, :, lo : lo + n]
-        )
+        if i or p:
+            inner = dot_nn(here[i], own[across, :, lo : lo + n])
+        else:
+            inner = out_v[0:size, lo : lo + n]
+        inner = inner + dot_nn(there[i], other[1 - side, :, lo : lo + n])
         rest = inner - means[i] * moment[:, share + lo : share + lo + n]
         most = jnp.max(jnp.abs(rest), axis=0, keepdims=True)
         step = jnp.maximum(most * (1.0 / 32767.0), 1e-30)
@@ -335,36 +387,21 @@
             copy.start()
 
     late = n_groups - 1
+    held = []
     for i in range(late):
         meet(i)
         for p in range(len(pieces)):
             code(i, p)
-            if i or p < AHEAD:
+            if i * len(pieces) + p < AHEAD:
                 send(i, p)
+            else:
+                held.append((i, p))
     meet(late)
+
     here_all = jnp.concatenate(here, axis=0)
     there_all = jnp.concatenate(there, axis=0)
-    mean_all = jnp.concatenate(means, axis=0)
-    pair = dot_nt(here_all, here_all) + dot_nt(there_all, there_all)
-    corners = [(r, c) for r in range(steps) for c in range(r, steps)]
-    half = len(corners) // 2
-
-    def corner(r, c):
-        return pair[r * count : (r + 1) * count, c * count : (c + 1) * count]
-
-    for k, (r, c) in enumerate(corners):
-        pair_send[k // half, k % half, :, 0:count] = corner(r, c)
-        pair_send[k // half, k % half, :, count : count + 1] = mean_all[
-            r * count : (r + 1) * count
-        ]
-    pair_copy = pltpu.make_async_remote_copy(
-        src_ref=pair_send.at[core], dst_ref=pair_recv.at[0], send_sem=q_send, recv_sem=q_recv,
-        device_id=(g, across), device_id_type=MESH,
-    )
-    pair_copy.start()
-    if late:
-        for p in range(AHEAD, len(pieces)):
-            send(0, p)
+    for i, p in held:
+        send(i, p)
     for p in range(len(pieces)):
         code(late, p)
         send(late, p)
@@ -372,23 +409,30 @@
         a, b = own[o, :, lo : lo + n], other[side, :, lo : lo + n]
         local[:, lo : lo + n] = dot_nn(here_all, a) + dot_nn(there_all, b)
         own_squares[:, lo : lo + n] = squares_of(a) + squares_of(b)
-    pair_copy.wait_recv()
-    half_copy = pltpu.make_async_remote_copy(
-        src_ref=pair_recv.at[0], dst_ref=pair_recv.at[1], send_sem=h_send, recv_sem=h_recv,
-        device_id=(g, mate), device_id_type=MESH,
-    )
-    half_copy.start()
-    half_copy.wait_recv()
+    half_copies = []
+    for i in range(n_groups):
+        pair_copies[i].wait_recv()
+        half_copy = pltpu.make_async_remote_copy(
+            src_ref=pair_recvs[i].at[0], dst_ref=pair_recvs[i].at[1],
+            send_sem=h_send.at[i], recv_sem=h_recv.at[i],
+            device_id=(g, mate), device_id_type=MESH,
+        )
+        half_copy.start()
+        half_copies.append(half_copy)
     wide = aug.shape[1]
     aug[...] = jnp.zeros((rank, wide), F32)
-    far_means = [None] * steps
-    for k, (r, c) in enumerate(corners):
-        which = core if k < half else 1 - core
-        far = pair_recv[which, k % half]
-        aug[r * count : (r + 1) * count, 128 * c : 128 * c + count] = jnp.square(
-            (pair_send[k // half, k % half] + far)[:, 0:count] / orbitals_count
-        )
-        far_means[r] = far[:, count : count + 1]
+    far_means = []
+    for i in range(n_groups):
+        half_copies[i].wait_recv()
+        for h in range(2):
+            far = pair_recvs[i][core if h == 0 else 1 - core]
+            entries = jnp.square((pair_sends[i][h] + far)[:, 0:count] / orbitals_count)
+            for r in range(i + 1):
+                top = r * count + h * half
+                aug[top : top + half, 128 * i : 128 * i + count] = entries[
+                    r * half : (r + 1) * half
+                ]
+            far_means.append(far[i * half : (i + 1) * half, count : count + 1])
     far_mean = jnp.concatenate(far_means, axis=0)
 
     def lane_of(row):
@@ -432,85 +476,95 @@
     best = [None] * steps
     stores = []
     moment_copy.wait_recv()
+    whole_rows = orbitals_count * 1.0
+
+    def columns_of(i, lo, n):
+        top, size = groups[i]
+        inner = (
+            local[top : top + size, lo : lo + n]
+            + arrived[top : top + size, lo : lo + n].astype(jnp.int32).astype(F32)
+            * far_scales[:, i * share + lo : i * share + lo + n]
+            + far_mean[top : top + size] * far_moment[:, share + lo : share + lo + n]
+        )
+        return jnp.square(inner / whole_rows)
+
+    def settle(s, solved, diagonal, lo, n):
+        out_v[s * count : (s + 1) * count, lo : lo + n] = solved
+        diagonal = diagonal - jnp.sum(solved * solved, axis=0, keepdims=True)
+        top = jnp.max(diagonal, axis=1, keepdims=True)
+        best[s] = top if best[s] is None else jnp.maximum(best[s], top)
+        return diagonal
+
     for p, (lo, n) in enumerate(pieces):
-        for i in range(n_groups):
+        for i in range(late):
             for copy in travel[i, p]:
                 copy.wait_recv()
-        scale = jnp.concatenate(
-            [
-                jnp.broadcast_to(
-                    far_scales[:, i * share + lo : i * share + lo + n], (size, n)
-                )
-                for i, (_, size) in enumerate(groups)
-            ],
-            axis=0,
-        )
-        inner = (
-            local[:, lo : lo + n]
-            + arrived[:, lo : lo + n].astype(jnp.int32).astype(F32) * scale
-            + far_mean * far_moment[:, share + lo : share + lo + n]
-        )
-        columns = jnp.square(inner / orbitals_count)
         diagonal = jnp.square(
-            (own_squares[:, lo : lo + n] + far_moment[:, lo : lo + n]) / orbitals_count
-        )
-        for s in range(steps):
-            solved = dot_nn(inverse[s], columns[0 : (s + 1) * count], HIGHEST)
-            out_v[s * count : (s + 1) * count, lo : lo + n] = solved
-            diagonal = diagonal - jnp.sum(solved * solved, axis=0, keepdims=True)
-            top = jnp.max(diagonal, axis=1, keepdims=True)
-            best[s] = top if best[s] is None else jnp.maximum(best[s], top)
+            (own_squares[:, lo : lo + n] + far_moment[:, lo : lo + n]) / whole_rows
+        )
+        if late:
+            columns = jnp.concatenate([columns_of(i, lo, n) for i in range(late)], axis=0)
+            for s in range(late):
+                solved = dot_nn(inverse[s], columns[0 : (s + 1) * count], HIGHEST)
+                diagonal = settle(s, solved, diagonal, lo, n)
+            out_v[late * count : rank, lo : lo + n] = dot_nn(
+                inverse[late][:, 0 : late * count], columns, HIGHEST
+            )
+        diag_ref[:, lo : lo + n] = diagonal
+    for p, (lo, n) in enumerate(pieces):
+        for copy in travel[late, p]:
+            copy.wait_recv()
+        solved = dot_nn(
+            inverse[late][:, late * count : rank], columns_of(late, lo, n), HIGHEST
+        )
+        if late:
+            solved = solved + out_v[late * count : rank, lo : lo + n]
+        diag_ref[:, lo : lo + n] = settle(late, solved, diag_ref[:, lo : lo + n], lo, n)
         store = pltpu.make_async_copy(
             out_v.at[:, pl.ds(lo, n)], factor_hbm.at[:, pl.ds(lo, n)], out_sem.at[p]
         )
         store.start()
         stores.append(store)
-        diag_ref[:, lo : lo + n] = diagonal
     row8 = lax.broadcasted_iota(jnp.int32, (8, 128), 0)
     tile = jnp.zeros((8, 128), F32)
     for s in range(steps):
         tile = jnp.where(row8 == s, jnp.broadcast_to(best[s], (8, 128)), tile)
-    tile_mine[0] = tile
-    round_orb = []
-    for d in range(1, n_orb):
-        copy = pltpu.make_async_remote_copy(
-            src_ref=tile_mine.at[0], dst_ref=tile_orb.at[d],
-            send_sem=mo_send.at[d], recv_sem=mo_recv.at[d],
-            device_id=(g, lax.rem(o + d, n_orb)), device_id_type=MESH,
-        )
-        copy.start()
-        round_orb.append(copy)
-    for d in range(1, n_orb):
-        round_orb[d - 1].wait_recv()
-        tile = jnp.maximum(tile, tile_orb[d])
-    tile_mine[1] = tile
-    round_grid = []
-    for d in range(1, n_grid):
-        copy = pltpu.make_async_remote_copy(
-            src_ref=tile_mine.at[1], dst_ref=tile_grid.at[d],
-            send_sem=mg_send.at[d], recv_sem=mg_recv.at[d],
-            device_id=(lax.rem(g + d, n_grid), o), device_id_type=MESH,
-        )
-        copy.start()
-        round_grid.append(copy)
-    for d in range(1, n_grid):
-        round_grid[d - 1].wait_recv()
-        tile = jnp.maximum(tile, tile_grid[d])
+    if ONE_ROUND >= n_grid * n_orb:
+        stages = [reach]
+    else:
+        stages = [[x for x in reach if not x[0]], [x for x in reach if x[0]]]
+    rounds = []
+    for k, stage in enumerate(stages):
+        tile_mine[k] = tile
+        started = []
+        for dg, do in stage:
+            at = dg * n_orb + do
+            copy = pltpu.make_async_remote_copy(
+                src_ref=tile_mine.at[k], dst_ref=tile_far.at[at],
+                send_sem=mo_send.at[at], recv_sem=mo_recv.at[at],
+                device_id=far_device(dg, do), device_id_type=MESH,
+            )
+            copy.start()
+            started.append((at, copy))
+        for at, copy in reversed(started):
+            copy.wait_recv()
+            tile = jnp.maximum(tile, tile_far[at])
+        rounds += [copy for _, copy in started]
     peaks_ref[...] = tile
     for store in stores:
         store.wait()
     for i in range(n_groups):
-        for d in range(1, n_grid):
+        for d in others:
             target, copy = first(i, d)
             owned(i, target, copy.wait_send)
 
         def sent(i=i):
-            for d in range(1, n_grid):
+            for d in others:
                 second(i, d).wait_send()
 
         owned(i, g, sent)
 
-    for copy in crossing + swapping + [moment_copy, pair_copy, half_copy] + round_orb + round_grid:
+    for copy in crossing + swapping + [moment_copy] + pair_copies + half_copies + rounds:
         copy.wait_send()
     for pair_of in travel.values():
         for copy in pair_of:
@@ -531,10 +585,10 @@
         n_groups = len(groups)
         n_pieces = len(pieces_of(share))
         wide = steps * 128
-        corners = steps * (steps + 1) // 2
-        assert count < 128 and count % BLOCK == 0 and corners % 2 == 0
+        assert count < 128 and count % BLOCK == 0 and count % 16 == 0
         dma = pltpu.SemaphoreType.DMA
         vmem = pltpu.VMEM
+        corners = [vmem((2, (i + 1) * count // 2, 128), F32) for i in range(n_groups)]
         blocks = [vmem((r * tiles, size, 128), BF16) for r, size in cuts]
         factor, diagonal, peaks = pl.pallas_call(
             functools.partial(kernel, n_grid, n_orb, steps, depth * n_orb, plan),
@@ -568,21 +622,21 @@
                 vmem((1, 2 * share), F32),
                 vmem((rank, share), F32),
                 vmem((1, share), F32),
-                vmem((2, corners // 2, count, 128), F32),
-                vmem((2, corners // 2, count, 128), F32),
+                corners,
+                corners,
                 vmem((rank, wide), F32),
                 vmem((rank, share), F32),
                 vmem((2, 8, 128), F32),
-                vmem((n_orb, 8, 128), F32),
-                vmem((n_grid, 8, 128), F32),
+                vmem((n_grid * n_orb, 8, 128), F32),
                 dma, dma((n_orb,)), dma((n_pieces,)), dma((2,)), dma((2,)),
                 dma((n_groups, n_grid)), dma((n_groups, n_grid)),
                 dma((n_groups, n_grid)), dma((n_groups, n_grid)),
-                dma((n_groups,)), dma((n_groups,)), dma, dma, dma, dma,
+                dma((n_groups,)), dma((n_groups,)),
+                dma((n_groups,)), dma((n_groups,)), dma((n_groups,)), dma((n_groups,)),
                 dma((n_groups, n_pieces)), dma((n_groups, n_pieces)),
                 dma((n_groups, n_pieces)), dma((n_groups, n_pieces)),
                 dma, dma,
-                dma((n_orb,)), dma((n_orb,)), dma((n_grid,)), dma((n_grid,)),
+                dma((n_grid * n_orb,)), dma((n_grid * n_orb,)),
             ],
             compiler_params=pltpu.CompilerParams(
                 collective_id=0, has_side_effects=True, vmem_limit_bytes=46 * 1024 * 1024

time: 63.9 us -> 62.4 us (0.977)
  Pallas kernels: 60.5 us -> 58.9 us
    pallas_call x1, Pallas kernels: 60.5 us -> 58.9 us  [on_device(): pl.pallas_call(functools.partial(kernel, n_grid, n_orb, steps, depth * n_...]
where the time goes in v3:
time: 62.4 us; the launch traced here: 62.2 us
  Pallas kernels  58.9 us (94%)
  local copies, waits for them, and re-layouts  2.63 us (4%)
  between operations  0.64 us (1%)
    pallas_call x1, Pallas kernels, on_device(): pl.pallas_call(functools.partial(kernel, n_grid, n_orb, steps, depth * n_...  58.9 us
    unnamed x2, local copies, waits for them, and re-layouts  2 us

profile of v3, /device:TPU:0, one launch (start us, length us, event | category | flops | bytes accessed | tf_op | source)
XLA Modules:
  0.0 62.2 jit_solution(11423486284618037422)
XLA Ops:
  0.6 58.9 %shard_map.49 = (f32[288,2048]{1,0:T(8,128)S(1)}, f32[1,2048]{1,0:T(1,128)S(1)}, f32[8,128]{1,0:T(8,128)S(1)}) custom-call(bf16[450,8192]{1,0:T(8,128)(2,1)} %orb_hbm.1, s32[3,96]{1,0:T(4,128)} %piv_hbm.1), custom_call_target="tpu_custom_call" | custom-call | tf_op jit(solution)/shard_map/pallas_call | solution.py:593
  59.6 0.6 %slice_reduce_fusion = f32[3]{0:T(128)} fusion(f32[8,128]{1,0:T(8,128)S(1)} %get-tuple-element.8), kind=kLoop, calls=%fused_computation | loop fusion | bytes 24 | tf_op jit(solution)/shard_map/slice | solution.py:648
  60.2 1.4 %copy.7 = f32[2048,288]{0,1:T(8,128)} copy(f32[2048,288]{0,1:T(8,128)S(1)} %bitcast.2) | data formatting | bytes 4718592
  61.6 0.6 copy.8

commit v4 on v3

--- a/solution.py
+++ b/solution.py
@@ -320,8 +320,6 @@
         if i == 0:
             lo, n = pieces[0]
             out_v[0 : groups[0][1], lo : lo + n] = dot_nn(here[0], own[across, :, lo : lo + n])
-        if i + 2 < n_groups:
-            add_up(i + 2)
         copy.wait_recv()
         there.append(gathered(i, swaps[i]))
         means.append(
@@ -396,6 +394,8 @@
                 send(i, p)
             else:
                 held.append((i, p))
+            if p == 0 and i + 2 < n_groups:
+                add_up(i + 2)
     meet(late)
 
     here_all = jnp.concatenate(here, axis=0)

time: 62.4 us -> 61.6 us (0.987)
  Pallas kernels: 58.9 us -> 58.2 us
    pallas_call x1, Pallas kernels: 58.9 us -> 58.2 us  [on_device(): pl.pallas_call(functools.partial(kernel, n_grid, n_orb, steps, depth * n_...]
where the time goes in v4:
time: 61.6 us; the launch traced here: 61.4 us
  Pallas kernels  58.2 us (94%)
  local copies, waits for them, and re-layouts  2.63 us (4%)
  between operations  0.64 us (1%)
    pallas_call x1, Pallas kernels, on_device(): pl.pallas_call(functools.partial(kernel, n_grid, n_orb, steps, depth * n_...  58.2 us
    unnamed x2, local copies, waits for them, and re-layouts  2 us

profile of v4, /device:TPU:0, one launch (start us, length us, event | category | flops | bytes accessed | tf_op | source)
XLA Modules:
  0.0 61.4 jit_solution(5053083694466255078)
XLA Ops:
  0.6 58.2 %shard_map.49 = (f32[288,2048]{1,0:T(8,128)S(1)}, f32[1,2048]{1,0:T(1,128)S(1)}, f32[8,128]{1,0:T(8,128)S(1)}) custom-call(bf16[450,8192]{1,0:T(8,128)(2,1)} %orb_hbm.1, s32[3,96]{1,0:T(4,128)} %piv_hbm.1), custom_call_target="tpu_custom_call" | custom-call | tf_op jit(solution)/shard_map/pallas_call | solution.py:593
  58.8 0.6 %slice_reduce_fusion = f32[3]{0:T(128)} fusion(f32[8,128]{1,0:T(8,128)S(1)} %get-tuple-element.8), kind=kLoop, calls=%fused_computation | loop fusion | bytes 24 | tf_op jit(solution)/shard_map/slice | solution.py:648
  59.4 1.4 %copy.7 = f32[2048,288]{0,1:T(8,128)} copy(f32[2048,288]{0,1:T(8,128)S(1)} %bitcast.2) | data formatting | bytes 4718592
  60.8 0.6 copy.8
